TPU v7x, 32 devices: a whole 2x2x4 slice. The times are simulated.
32 devices in a mesh: site: 2 (over y), pts: 16 (over z, x, core).
Axes of the slice: x: 2, y: 2, z: 4, core: 2. Of those that a mesh axis runs over, the one named last changes fastest.
Arguments:
- green_tensors: bfloat16 [512, 4, 6, 2, 1024], P(('site', 'pts')), parts along dimension 0, may hold values from -6 to 6
- block_lists: int32 [32, 32], P(('site', 'pts')), parts along dimension 0, may hold values from 0 to 255, as said below
- block_count: int32 [32], P(('site', 'pts')), parts along dimension 0, may hold values from 1 to 32
- onset_steps: int32 [32, 16, 128], P(('site', 'pts')), parts along dimension 0, may hold values from 0 to 255
- slip_amount: float32 [32, 16, 128], P(('site', 'pts')), parts along dimension 0, may hold values from 0.2 to 2
- mechanism: float32 [32, 6], P(('site', 'pts')), parts along dimension 0, may hold values from -2.4 to 2.4
- slip_rate: float32 [32, 16, 128], P(('site', 'pts')), parts along dimension 0, may hold values from 0.005 to 0.05
Outputs:
- seismograms: float32 [32, 16, 2, 1024], P(('site', 'pts')), parts along dimension 0
There are 2 independent parts, one for each index of `site`. A program takes and returns all parts, laid end to end along the dimension named above; each array names one. Nothing has to cross between parts.
Inputs may be any that keep to these rules, and one draw needn't show every extreme that they name: `block_lists`: numbers of point blocks; the ruptures held by one device name at most 2 entries in blocks held by any one device, and exactly 2 for some holder.
All inputs are finite; a program needn't handle non-finite values.
Results may differ from a plain program's by a relative error of at most 0.0003.
Values may be sent and summed in bfloat16 or wider, within the bound.
A program may use at most 128 MiB of HBM per device.

v0:
```python
import jax
import jax.numpy as jnp
from jax import lax
from jax.sharding import PartitionSpec as P

MAXON = 256


def lag_traces(traces, onsets):
    length = traces.shape[-1]
    shifted_all = traces
    for bit_index in range((MAXON - 1).bit_length()):
        stride = 1 << bit_index
        shifted = jnp.pad(shifted_all, ((0, 0), (0, 0), (stride, 0)))[:, :, :length]
        bit_set = jnp.bitwise_and(jnp.right_shift(onsets, bit_index), 1) == 1
        shifted_all = jnp.where(bit_set[:, None, None], shifted, shifted_all)
    return shifted_all


def weighted_sum(traces, weights, onsets):

    def per_variation(weight_row, onset_row):
        return jnp.sum(weight_row[:, None, None] * lag_traces(traces, onset_row), axis=0)

    return jax.vmap(per_variation)(weights, onsets)


def convolve_rate(motion, slip_rate):
    taps = slip_rate.shape[-1]
    length = motion.shape[-1]
    offset = jnp.arange(taps, dtype=jnp.int32)[None, :] - jnp.arange(taps, dtype=jnp.int32)[:, None]
    near = jnp.where(offset >= 0, jnp.take(slip_rate, jnp.clip(offset, 0, taps - 1), axis=-1), 0.0)
    far = jnp.where(
        offset < 0, jnp.take(slip_rate, jnp.clip(offset + taps, 0, taps - 1), axis=-1), 0.0
    )
    blocked = motion.reshape(motion.shape[:-1] + (length // taps, taps))
    earlier = jnp.pad(blocked, ((0, 0), (0, 0), (0, 0), (1, 0), (0, 0)))[:, :, :, :-1, :]
    result = jnp.einsum("rvcbi,rvij->rvcbj", blocked, near, precision=lax.Precision.HIGHEST)
    result = result + jnp.einsum("rvcbi,rvij->rvcbj", earlier, far, precision=lax.Precision.HIGHEST)
    return result.reshape(motion.shape)


def local(green_tensors, block_lists, block_count, onset_steps, slip_amount, mechanism, slip_rate):
    held = green_tensors.shape[0]
    points = green_tensors.shape[1]
    length = green_tensors.shape[-1]
    ruptures, listed = block_lists.shape
    devices = lax.axis_size("pts")
    capacity = max(1, ruptures * listed // devices)
    own_index = lax.axis_index("pts")
    entries = ruptures * listed
    every_list = lax.all_gather(block_lists, "pts", axis=0, tiled=True)
    holder = every_list // held
    local_block = every_list % held
    order = jnp.arange(entries, dtype=jnp.int32)
    earlier_same = (holder[:, :, None] == holder[:, None, :]) & (
        order[None, None, :] < order[None, :, None]
    )
    slot_rank = jnp.sum(earlier_same.astype(jnp.int32), axis=2)
    slot_ids = jnp.arange(capacity, dtype=jnp.int32)
    chosen = (
        (holder == own_index)[:, None, :] & (slot_rank[:, None, :] == slot_ids[None, :, None])
    ).astype(jnp.int32)
    slot_block = jnp.sum(chosen * local_block[:, None, :], axis=2)
    my_holder = block_lists.reshape(entries) // held
    my_rank = lax.dynamic_index_in_dim(slot_rank, own_index, 0, keepdims=False)
    source_row = my_holder * capacity + my_rank
    kept_mask = (jnp.arange(listed, dtype=jnp.int32)[None, :] < block_count[:, None]).astype(
        jnp.float32
    )
    weights = slip_amount * jnp.repeat(kept_mask, points, axis=1)[:, None, :]

    def rupture_motion(inputs):
        rupture_traces, weight_rows, onset_rows = inputs
        return weighted_sum(rupture_traces.reshape(-1, 2, length), weight_rows, onset_rows)

    outgoing = jnp.take(green_tensors, slot_block.reshape(-1), axis=0)
    outgoing = outgoing.reshape((devices, capacity) + green_tensors.shape[1:])
    incoming = lax.all_to_all(outgoing, "pts", split_axis=0, concat_axis=0, tiled=True)
    flat_rows = incoming.reshape((devices * capacity,) + green_tensors.shape[1:])
    needed = jnp.take(flat_rows, source_row, axis=0)
    traces = jnp.einsum(
        "rkpsct,rs->rkpct",
        needed.reshape((ruptures, listed) + green_tensors.shape[1:]).astype(jnp.float32),
        mechanism,
        precision=lax.Precision.HIGHEST,
    )
    motion = lax.map(rupture_motion, (traces, weights, onset_steps))
    return convolve_rate(motion, slip_rate)


def solution(mesh):
    in_specs = (
        P(("site", "pts"), None, None, None, None),
        P(("site", "pts"), None),
        P(("site", "pts")),
        P(("site", "pts"), None, None),
        P(("site", "pts"), None, None),
        P(("site", "pts"), None),
        P(("site", "pts"), None, None),
    )
    out_specs = P(("site", "pts"), None, None, None)
    return jax.shard_map(local, mesh=mesh, in_specs=in_specs, out_specs=out_specs, check_vma=False)
```

profile of v0, /device:TPU:0, one launch (start us, length us, event | category | flops | bytes accessed | tf_op | source)
XLA Modules:
  0.0 280.7 jit_solution(6019575131359495665)
XLA Ops:
  0.0 0.0 copy-start
  0.0 23.4 %all-gather = s32[16,1,32]{2,1,0:T(1,128)S(1)} all-gather(s32[1,1,32]{2,1,0:T(1,128)} %bitcast.123), channel_id=1, replica_groups=mesh['site'=2,'pts'=16] {'pts'}, dimensions={0}, use_global_device_ids=true | all-gather | bytes 2176 | tf_op jit(solution)/shard_map/all_gather | solution.py:52
  23.4 0.5 convert_reduce_fusion
  23.9 0.1 select_reduce_fusion
  24.0 0.1 copy.21
  24.1 0.1 reshape.339
  24.2 0.1 copy.20
  24.3 0.0 copy-done
  24.3 0.0 copy-start.2
  24.3 8.4 %gather_fusion = bf16[32,4,6,2,1024]{4,3,2,1,0:T(2,128)(2,1)} fusion(bf16[16,4,6,2,1024]{4,3,2,1,0:T(2,128)(2,1)S(1)} %copy-done, s32[1024]{0:T(1024)S(1)} %pad_clamp_fusion.1), kind=kCustom, calls=%fused_computation.2 | custom fusion | bytes 6291584 | tf_op jit(solution)/shard_map/jit(_take)/gather | solution.py:77
  32.7 6.5 %broadcast_select_fusion.2 = bf16[16,2,4,6,2,1024]{5,4,3,2,1,0:T(2,128)(2,1)} fusion(bf16[16,2,4,6,2,1024]{5,4,3,2,1,0:T(2,128)(2,1)} %bitcast.116, pred[16,2]{1,0:T(8,128)(4,1)S(1)} %copy.20), kind=kLoop, calls=%fused_computation.22 | loop fusion | flops 1572864 | bytes 6291488 | tf_op jit(solution)/shard_map/jit(_take)/select_n | solution.py:77
  39.2 4.7 %all-to-all-start = ((bf16[16,2,4,6,2,1024]{5,4,3,2,1,0:T(2,128)(2,1)}), bf16[16,2,4,6,2,1024]{5,4,3,2,1,0:T(2,128)(2,1)}, u32[]{:S(2)}, u32[]{:S(2)}) async-start(bf16[16,2,4,6,2,1024]{5,4,3,2,1,0:T(2,128)(2,1)} %broadcast_select_fusion.2), calls=%async_computation | async-start | bytes 6291456 | tf_op jit(solution)/shard_map/all_to_all | solution.py:79
  44.5 0.1 broadcast_in_dim.160
  44.6 0.1 broadcast_in_dim.161
  44.7 0.0 copy-done.2
  44.7 0.1 copy.22
  44.8 54.8 %gather_fusion.2 = f32[16384,16]{1,0:T(8,128)} fusion(f32[16,128]{0,1:T(8,128)S(1)} %bitcast.113, s32[16384]{0:T(1024)S(1)} %bitcast_clamp_fusion.1), kind=kCustom, calls=%fused_computation.clone | custom fusion | bytes 2162688 | tf_op jit(solution)/shard_map/jit(_take)/gather | solution.py:32
  99.6 5.2 %copy.23 = f32[128,128,16]{1,0,2:T(8,128)S(1)} copy(f32[128,128,16]{2,1,0:T(8,128)} %bitcast.118) | data formatting | bytes 2097152 | tf_op jit(solution)/shard_map/jit(_take)/gather | solution.py:32
  104.9 0.0 copy-start.5
  104.9 0.0 copy-start.4
  104.9 0.0 copy-start.3
  104.9 54.8 %gather_fusion.3 = f32[16384,16]{1,0:T(8,128)} fusion(f32[16,128]{0,1:T(8,128)S(1)} %bitcast.114, s32[16384]{0:T(1024)S(1)} %bitcast_clamp_fusion), kind=kCustom, calls=%fused_computation.1.clone | custom fusion | bytes 2162688 | tf_op jit(solution)/shard_map/jit(_take)/gather | solution.py:34
  159.7 6.1 %copy.25 = f32[128,128,16]{1,0,2:T(8,128)} copy(f32[128,128,16]{2,1,0:T(8,128)} %bitcast.117) | data formatting | bytes 2097152 | tf_op jit(solution)/shard_map/jit(_take)/gather | solution.py:34
  165.7 0.0 copy-done.5
  165.9 0.0 copy-done.4
  165.9 0.0 copy-done.3
  165.9 0.0 all-to-all-done
  166.0 10.3 %gather_fusion.1 = bf16[32,4,6,2,1024]{4,3,2,1,0:T(2,128)(2,1)} fusion(bf16[32,4,6,2,1024]{4,3,2,1,0:T(2,128)(2,1)} %bitcast.16, s32[1024]{0:T(1024)S(1)} %pad_clamp_fusion), kind=kCustom, calls=%fused_computation.3 | custom fusion | bytes 6291584 | tf_op jit(solution)/shard_map/jit(_take)/gather | solution.py:81
  176.2 4.7 %broadcast_select_fusion.1 = bf16[32,4,6,2,1024]{4,3,2,1,0:T(2,128)(2,1)S(1)} fusion(bf16[32,4,6,2,1024]{4,3,2,1,0:T(2,128)(2,1)} %gather_fusion.1, pred[32]{0:T(512)(128)(4,1)S(1)} %compare_and_fusion.1), kind=kLoop, calls=%fused_computation.21 | loop fusion | flops 1572864 | bytes 6291488 | tf_op jit(solution)/shard_map/jit(_take)/select_n | solution.py:81
  181.0 0.0 copy-done.6
  181.0 3.6 %fusion.9 = f32[1,128,2,1024]{3,0,2,1:T(1,128)S(1)} fusion(bf16[128,2,1024,6]{2,1,3,0:T(2,128)(2,1)S(1)} %bitcast.115, f32[1,6]{1,0:T(1,128)S(1)} %copy-done.6), kind=kOutput, calls=%fused_computation.23 | convolution fusion | flops 18874368 | bytes 4194328 | tf_op jit(solution)/shard_map/rkpsct,rs->rkpct/dot_general | solution.py:82
  184.6 0.3 copy.34
  184.9 0.3 pad_slice_fusion.7
  185.3 6.9 %broadcast_select_fusion = f32[16,128,2,1024]{3,1,2,0:T(8,128)} fusion(f32[128,2,1024]{2,0,1:T(8,128)S(1)} %bitcast.120, f32[128,2,1024]{2,0,1:T(8,128)S(1)} %pad_slice_fusion.7, pred[16,128]{1,0:T(8,128)(4,1)S(1)} %get-tuple-element.29), kind=kLoop, calls=%fused_computation.20 | loop fusion | flops 4194304 | bytes 18876416 | tf_op jit(solution)/shard_map/while/body/eval_jaxpr/vmap(jit(_where))/select_n | solution.py:16
  192.2 14.9 %fusion = f32[16,128,2,1024]{3,1,2,0:T(8,128)S(1)} fusion(f32[16,128,2,1024]{3,1,2,0:T(8,128)} %broadcast_select_fusion, pred[16,128]{1,0:T(8,128)(4,1)S(1)} %get-tuple-element.30), kind=kLoop, calls=%fused_computation.11 | loop fusion | flops 4194304 | bytes 33556480 | tf_op jit(solution)/shard_map/while/body/eval_jaxpr/vmap(jit(_where))/select_n | solution.py:16
  207.1 8.4 %fusion.1 = f32[16,128,2,1024]{3,1,2,0:T(8,128)} fusion(f32[16,128,2,1024]{3,1,2,0:T(8,128)S(1)} %fusion, pred[16,128]{1,0:T(8,128)(4,1)S(1)} %get-tuple-element.24), kind=kLoop, calls=%fused_computation.12 | loop fusion | flops 4194304 | bytes 33556480 | tf_op jit(solution)/shard_map/while/body/eval_jaxpr/vmap(jit(_where))/select_n | solution.py:16
  215.4 14.9 %fusion.2 = f32[16,128,2,1024]{3,1,2,0:T(8,128)S(1)} fusion(f32[16,128,2,1024]{3,1,2,0:T(8,128)} %fusion.1, pred[16,128]{1,0:T(8,128)(4,1)S(1)} %get-tuple-element.25), kind=kLoop, calls=%fused_computation.13 | loop fusion | flops 4194304 | bytes 33556480 | tf_op jit(solution)/shard_map/while/body/eval_jaxpr/vmap(jit(_where))/select_n | solution.py:16
  230.3 8.4 %fusion.3 = f32[16,128,2,1024]{3,1,2,0:T(8,128)} fusion(f32[16,128,2,1024]{3,1,2,0:T(8,128)S(1)} %fusion.2, pred[16,128]{1,0:T(8,128)(4,1)S(1)} %get-tuple-element.26), kind=kLoop, calls=%fused_computation.14 | loop fusion | flops 4194304 | bytes 33556480 | tf_op jit(solution)/shard_map/while/body/eval_jaxpr/vmap(jit(_where))/select_n | solution.py:16
  238.7 19.1 %fusion.4 = f32[16,128,2,1024]{3,1,2,0:T(8,128)} fusion(f32[16,128,2,1024]{3,1,2,0:T(8,128)} %fusion.3, pred[16,128]{1,0:T(8,128)(4,1)S(1)} %get-tuple-element.27), kind=kLoop, calls=%fused_computation.15 | loop fusion | flops 4194304 | bytes 33556480 | tf_op jit(solution)/shard_map/while/body/eval_jaxpr/vmap(jit(_where))/select_n | solution.py:16
  257.8 14.9 %fusion.5 = f32[16,128,2,1024]{3,1,2,0:T(8,128)S(1)} fusion(f32[16,128,2,1024]{3,1,2,0:T(8,128)} %fusion.4, pred[16,128]{1,0:T(8,128)(4,1)S(1)} %get-tuple-element.28), kind=kLoop, calls=%fused_computation.16 | loop fusion | flops 4194304 | bytes 33556480 | tf_op jit(solution)/shard_map/while/body/eval_jaxpr/vmap(jit(_where))/select_n | solution.py:16
  272.7 0.0 copy-start.1
  272.7 3.7 %fusion.8 = f32[16,2,1024]{2,1,0:T(2,128)S(1)} fusion(f32[16,128,2,1024]{3,1,2,0:T(8,128)S(1)} %fusion.5, f32[16,128]{1,0:T(8,128)S(1)} %multiply_bitcast_fusion, pred[16,128]{1,0:T(8,128)(4,1)S(1)} %get-tuple-element.22), kind=kLoop, calls=%fused_computation.19 | loop fusion | flops 12550144 | bytes 16918528 | tf_op jit(solution)/shard_map/while/body/eval_jaxpr/vmap()/reduce_sum | solution.py:23
  276.4 0.1 reshape.343
  276.5 0.1 reshape.345
  276.6 1.0 fusion.14
  277.7 2.3 convolution_add_fusion
  279.9 0.7 reshape.348
  280.7 0.0 copy-done.1
  (17 shorter events, 0.3 us)
Async XLA Ops:
  0.0 24.3 %copy-start = (bf16[16,4,6,2,1024]{4,3,2,1,0:T(2,128)(2,1)S(1)}, bf16[16,4,6,2,1024]{4,3,2,1,0:T(2,128)(2,1)}, u32[]{:S(2)}) copy-start(bf16[16,4,6,2,1024]{4,3,2,1,0:T(2,128)(2,1)} %param.9) | copy-start | bytes 4718596
  24.3 20.4 %copy-start.2 = (f32[1,16,128]{2,1,0:T(8,128)S(1)}, f32[1,16,128]{2,1,0:T(8,128)}, u32[]{:S(2)}) copy-start(f32[1,16,128]{2,1,0:T(8,128)} %param.15) | copy-start | bytes 24580
  39.2 126.8 %all-to-all-start = ((bf16[16,2,4,6,2,1024]{5,4,3,2,1,0:T(2,128)(2,1)}), bf16[16,2,4,6,2,1024]{5,4,3,2,1,0:T(2,128)(2,1)}, u32[]{:S(2)}, u32[]{:S(2)}) async-start(bf16[16,2,4,6,2,1024]{5,4,3,2,1,0:T(2,128)(2,1)} %broadcast_select_fusion.2), calls=%async_computation | async-start | bytes 6291456 | tf_op jit(solution)/shard_map/all_to_all | solution.py:79
  104.9 60.9 %copy-start.5 = (s32[1,32]{1,0:T(1,128)S(1)}, s32[1,32]{1,0:T(1,128)}, u32[]{:S(2)}) copy-start(s32[1,32]{1,0:T(1,128)} %param.10) | copy-start | bytes 388
  104.9 61.0 %copy-start.4 = (f32[1,16,128]{2,1,0:T(8,128)S(1)}, f32[1,16,128]{2,1,0:T(8,128)}, u32[]{:S(2)}) copy-start(f32[1,16,128]{2,1,0:T(8,128)} %param.13) | copy-start | bytes 24580
  104.9 61.0 %copy-start.3 = (s32[1,16,128]{2,1,0:T(8,128)S(1)}, s32[1,16,128]{2,1,0:T(8,128)}, u32[]{:S(2)}) copy-start(s32[1,16,128]{2,1,0:T(8,128)} %param.12) | copy-start | bytes 24580
  165.7 15.2 %copy-start.6 = (f32[1,6]{1,0:T(1,128)S(1)}, f32[1,6]{1,0:T(1,128)}, u32[]{:S(2)}) copy-start(f32[1,6]{1,0:T(1,128)} %param.14) | copy-start | bytes 76
  272.7 8.0 %copy-start.1 = (bf16[16,4,6,2,1024]{4,3,2,1,0:T(2,128)(2,1)S(1)}, bf16[16,4,6,2,1024]{4,3,2,1,0:T(2,128)(2,1)}, u32[]{:S(2)}) copy-start(bf16[16,4,6,2,1024]{4,3,2,1,0:T(2,128)(2,1)} %param.9) | copy-start | bytes 4718596
where the time goes:
time: 281 us
  local copies, waits for them, and re-layouts  142 us (51%)
  other arithmetic  103 us (37%)
  blocking collectives  23.4 us (8%)
  matrix products  6.9 us (2%)
  starting transfers between devices  4.69 us (2%)
    select_n x7, other arithmetic, lag_traces(): shifted_all = jnp.where(bit_set[:, None, None], shifted, shifted_all)  87.4 us
    gather x2, local copies, waits for them, and re-layouts, convolve_rate(): jnp.take(slip_rate, jnp.clip(offset + taps, 0, taps - 1), axis=-1)  60.8 us
    gather x2, local copies, waits for them, and re-layouts, convolve_rate(): jnp.take(slip_rate, jnp.clip(offset, 0, taps - 1), axis=-1)  60 us
    all_gather x1, blocking collectives, local(): every_list = lax.all_gather(block_lists, 'pts', axis=0, tiled=True)  23.4 us
    gather x1, local copies, waits for them, and re-layouts, local(): needed = jnp.take(flat_rows, source_row, axis=0)  10.3 us
    gather x1, local copies, waits for them, and re-layouts, local(): outgoing = jnp.take(green_tensors, slot_block.reshape(-1), axis=0)  8.37 us
    select_n x2, other arithmetic, local(): outgoing = jnp.take(green_tensors, slot_block.reshape(-1), axis=0)  6.45 us
  transfers between devices with their start and end apart: 1, of which 0 were waited for; matrix products, arithmetic and copies ran while one was open for 43% of the time, Pallas kernels for 0%

commit v1 on v0

v1 whole, which is shorter than its diff:
```python
import functools

import jax
import jax.numpy as jnp
from jax import lax
from jax.experimental import pallas as pl
from jax.experimental.pallas import tpu as pltpu
from jax.sharding import PartitionSpec as P

LANES = 128


def exchange_kernel(n, cap, width, wants_ref, mech_ref, green_ref, out_ref,
                    wanted, mechs, wanted_s, outbox, send_w, recv_w, send_m, recv_m,
                    local_sem, send_t, recv_t):
    me = lax.axis_index("pts")

    barrier = pltpu.get_barrier_semaphore()

    def greet(d, carry):
        pl.semaphore_signal(barrier, inc=1, device_id={"pts": lax.rem(me + d, n)},
                            device_id_type=pl.DeviceIdType.MESH)
        return carry

    lax.fori_loop(1, n, greet, 0)
    pl.semaphore_wait(barrier, n - 1)

    def want_copy(d):
        peer = lax.rem(me + d, n)
        return pltpu.make_async_remote_copy(
            src_ref=wants_ref.at[peer], dst_ref=wanted.at[n - d],
            send_sem=send_w.at[d], recv_sem=recv_w.at[n - d],
            device_id={"pts": peer}, device_id_type=pl.DeviceIdType.MESH)

    def mech_copy(d):
        peer = lax.rem(me + d, n)
        return pltpu.make_async_remote_copy(
            src_ref=mech_ref, dst_ref=mechs.at[n - d],
            send_sem=send_m.at[d], recv_sem=recv_m.at[n - d],
            device_id={"pts": peer}, device_id_type=pl.DeviceIdType.MESH)

    def start_meta(d, carry):
        want_copy(d).start()
        mech_copy(d).start()
        return carry

    lax.fori_loop(1, n, start_meta, 0)
    wanted[0] = wants_ref[me]
    mechs[0] = mech_ref[...]

    def wait_meta(d, carry):
        want_copy(d).wait()
        mech_copy(d).wait()
        return carry

    lax.fori_loop(1, n, wait_meta, 0)
    to_scalar = pltpu.make_async_copy(wanted, wanted_s, local_sem)
    to_scalar.start()
    to_scalar.wait()

    def traces_for(d, slot):
        lhs = mechs[d][:, :width]
        high = lhs.astype(jnp.bfloat16).astype(jnp.float32)
        rest = lhs - high
        mid = rest.astype(jnp.bfloat16).astype(jnp.float32)
        stack = jnp.concatenate([high, mid, rest - mid], axis=0).astype(jnp.bfloat16)
        block = green_ref[wanted_s[d, 0, slot]]
        parts = jnp.dot(stack, block, preferred_element_type=jnp.float32)
        m = lhs.shape[0]
        return parts[0:m] + (parts[m:2 * m] + parts[2 * m:3 * m])

    def trace_copy(d):
        peer = lax.rem(me + d, n)
        return pltpu.make_async_remote_copy(
            src_ref=outbox.at[d], dst_ref=out_ref.at[me],
            send_sem=send_t.at[d], recv_sem=recv_t.at[n - d],
            device_id={"pts": peer}, device_id_type=pl.DeviceIdType.MESH)

    def step(d, carry):
        for slot in range(cap):
            outbox[d, slot] = traces_for(d, slot)

        @pl.when(d > 1)
        def _():
            trace_copy(d - 1).start()

        return carry

    lax.fori_loop(1, n, step, 0)
    for slot in range(cap):
        out_ref[me, slot] = traces_for(0, slot)
    trace_copy(n - 1).start()

    def wait_traces(d, carry):
        trace_copy(d).wait()
        return carry

    lax.fori_loop(1, n, wait_traces, 0)


def motion_kernel(points, comps, rows_ref, count_ref, traces_ref, onset_ref, slip_ref, rate_ref,
                  out_ref, motion):
    variations = onset_ref.shape[0]
    length = traces_ref.shape[-1]
    tiles = length // LANES
    lane = lax.broadcasted_iota(jnp.int32, (8, LANES), 1)
    motion[0:comps] = jnp.zeros((comps,) + motion.shape[1:], jnp.float32)
    for group in range(variations // 8):
        onsets = onset_ref[group * 8:group * 8 + 8, :]
        slips = slip_ref[group * 8:group * 8 + 8, :]

        def body(k, acc):
            acc = list(acc)
            row = rows_ref[k]
            for p in range(points):
                pick = jnp.full((8, LANES), k * points + p, jnp.int32)
                onset = jnp.take_along_axis(onsets, pick, axis=1)
                slip = jnp.take_along_axis(slips, pick, axis=1)
                shift = jnp.bitwise_and(onset, LANES - 1)
                back = jnp.right_shift(onset, 7) + (lane >= LANES - shift).astype(jnp.int32)
                one = back >= 1
                two = back >= 2
                source = jnp.bitwise_and(lane - shift, LANES - 1)
                for c in range(comps):
                    prev2 = jnp.zeros((8, LANES), jnp.float32)
                    prev1 = prev2
                    for i in range(tiles):
                        cur = jnp.broadcast_to(
                            traces_ref[row, pl.ds(p * comps + c, 1), i * LANES:(i + 1) * LANES],
                            (8, LANES))
                        mixed = jnp.where(two, prev2, jnp.where(one, prev1, cur))
                        acc[i * comps + c] += slip * jnp.take_along_axis(mixed, source, axis=1)
                        prev2, prev1 = prev1, cur
            return tuple(acc)

        zero = jnp.zeros((8, LANES), jnp.float32)
        acc = lax.fori_loop(0, count_ref[0], body, (zero,) * (tiles * comps))
        for j in range(tiles * comps):
            motion[comps + j, group * 8:group * 8 + 8, :] = acc[j]

    count = tiles * comps
    i_row = lax.broadcasted_iota(jnp.int32, (LANES, LANES), 0)
    j_lane = lax.broadcasted_iota(jnp.int32, (LANES, LANES), 1)
    near_mask = j_lane >= i_row
    for v in range(variations):
        rate = jnp.broadcast_to(rate_ref[v:v + 1, :], (LANES, LANES))
        turned = pltpu.roll(rate, 0, 1, stride=1, stride_axis=0)
        both = jnp.concatenate(
            [jnp.where(near_mask, turned, 0.0), jnp.where(near_mask, 0.0, turned)], axis=0)
        here = motion[comps:comps + count, v, :]
        before = motion[0:count, v, :]
        lhs = jnp.concatenate([here, before], axis=1)
        result = jnp.dot(lhs, both, precision=lax.Precision.HIGHEST,
                         preferred_element_type=jnp.float32)
        for i in range(tiles):
            out_ref[v, :, i * LANES:(i + 1) * LANES] = result[i * comps:(i + 1) * comps, :]


def local(green_tensors, block_lists, block_count, onset_steps, slip_amount, mechanism, slip_rate):
    held, points, strains, comps, length = green_tensors.shape
    ruptures, listed = block_lists.shape
    assert ruptures == 1
    variations = onset_steps.shape[1]
    n = lax.axis_size("pts")
    cap = max(1, listed // n)
    width = points * strains * comps
    rows_per = points * comps

    blocks = block_lists.reshape(listed)
    holder = blocks // held
    local_block = blocks % held
    order = jnp.arange(listed, dtype=jnp.int32)
    rank = jnp.sum(((holder[:, None] == holder[None, :]) & (order[None, :] < order[:, None]))
                   .astype(jnp.int32), axis=1)
    place = holder * cap + rank
    lanes = jnp.arange(LANES, dtype=jnp.int32)
    hit = (holder[None, None, :] == jnp.arange(n, dtype=jnp.int32)[:, None, None]) & (
        rank[None, None, :] == lanes[None, :, None])
    wants = jnp.sum(jnp.where(hit, local_block[None, None, :], 0), axis=2).reshape(n, 1, LANES)

    out_row = jnp.arange(rows_per, dtype=jnp.int32)[:, None]
    in_row = jnp.arange(LANES, dtype=jnp.int32)[None, :]
    same = (in_row // (strains * comps) == out_row // comps) & (in_row % comps == out_row % comps)
    strain_of = (in_row // comps) % strains
    mech = jnp.zeros((rows_per, LANES), jnp.float32)
    for s in range(strains):
        mech = jnp.where(same & (strain_of == s), mechanism[0, s], mech)

    vmem = pl.BlockSpec(memory_space=pltpu.VMEM)
    smem = pl.BlockSpec(memory_space=pltpu.SMEM)
    traces = pl.pallas_call(
        functools.partial(exchange_kernel, n, cap, width),
        out_shape=jax.ShapeDtypeStruct((n, cap, rows_per, length), jnp.float32),
        in_specs=[vmem, vmem, vmem],
        out_specs=vmem,
        scratch_shapes=[
            pltpu.VMEM((n, 1, LANES), jnp.int32),
            pltpu.VMEM((n, rows_per, LANES), jnp.float32),
            pltpu.SMEM((n, 1, LANES), jnp.int32),
            pltpu.VMEM((n, cap, rows_per, length), jnp.float32),
            pltpu.SemaphoreType.DMA((n,)),
            pltpu.SemaphoreType.DMA((n,)),
            pltpu.SemaphoreType.DMA((n,)),
            pltpu.SemaphoreType.DMA((n,)),
            pltpu.SemaphoreType.DMA,
            pltpu.SemaphoreType.DMA((n,)),
            pltpu.SemaphoreType.DMA((n,)),
        ],
        compiler_params=pltpu.CompilerParams(
            collective_id=0, has_side_effects=True, vmem_limit_bytes=48 << 20),
        name="exchange",
    )(wants, mech, green_tensors.reshape(held, width, length))

    seismograms = pl.pallas_call(
        functools.partial(motion_kernel, points, comps),
        out_shape=jax.ShapeDtypeStruct((variations, comps, length), jnp.float32),
        in_specs=[smem, smem, vmem, vmem, vmem, vmem],
        out_specs=vmem,
        scratch_shapes=[pltpu.VMEM(((length // LANES + 1) * comps, variations, LANES), jnp.float32)],
        compiler_params=pltpu.CompilerParams(vmem_limit_bytes=48 << 20),
        name="motion",
    )(place, block_count, traces.reshape(n * cap, rows_per, length),
      onset_steps[0], slip_amount[0], slip_rate[0])
    return seismograms[None]


def solution(mesh):
    in_specs = (
        P(("site", "pts"), None, None, None, None),
        P(("site", "pts"), None),
        P(("site", "pts")),
        P(("site", "pts"), None, None),
        P(("site", "pts"), None, None),
        P(("site", "pts"), None),
        P(("site", "pts"), None, None),
    )
    out_specs = P(("site", "pts"), None, None, None)
    return jax.shard_map(local, mesh=mesh, in_specs=in_specs, out_specs=out_specs, check_vma=False)
```

time: 281 us -> 62.5 us (0.22)
  the two profiles are of different devices: /device:TPU:0 before, /device:TPU:15 now
where the time goes in v1:
time: 62.5 us; the launch traced here: 62.2 us
  Pallas kernels  51.8 us (83%)
  other arithmetic  5.64 us (9%)
  local copies, waits for them, and re-layouts  4.07 us (7%)
  between operations  0.76 us (1%)
    pallas_call x1, Pallas kernels, local(): pl.pallas_call(functools.partial(exchange_kernel, n, cap, width), out_sha...  34.8 us
    pallas_call x1, Pallas kernels, local(): pl.pallas_call(functools.partial(motion_kernel, points, comps), out_shape...  17 us
    select_n x1, other arithmetic, local(): mech = jnp.where(same & (strain_of == s), mechanism[0, s], mech)  3.83 us
    reshape x1, local copies, waits for them, and re-layouts, local(): green_tensors.reshape(held, width, length)  2.5 us
    slice x1, local copies, waits for them, and re-layouts, local(): mech = jnp.where(same & (strain_of == s), mechanism[0, s], mech)  1.55 us

profile of v1, /device:TPU:15, one launch (start us, length us, event | category | flops | bytes accessed | tf_op | source)
XLA Modules:
  0.0 62.2 jit_solution(13002986104026547929)
XLA Ops:
  0.7 0.7 %fusion.1 = s32[32]{0:T(128)S(1)} fusion(s32[1,32]{1,0:T(1,128)} %param.8), kind=kLoop, calls=%fused_computation.30 | loop fusion | flops 480 | bytes 256 | tf_op jit(solution)/shard_map/eq | solution.py:173
  1.3 0.7 %and_select_fusion.6 = (s32[32]{0:T(128)S(1)}, s32[32]{0:T(128)S(1)}) fusion(s32[1,32]{1,0:T(1,128)} %param.8), kind=kLoop, calls=%fused_computation.13 | loop fusion | flops 608 | bytes 384 | tf_op jit(solution)/shard_map/jit(remainder)/select_n | solution.py:171
  2.0 0.2 convert_reduce_fusion
  2.3 1.5 %fusion.2 = (f32[1,1]{1,0:T(1,128)}, f32[1,1]{1,0:T(1,128)}, f32[1,1]{1,0:T(1,128)}, f32[1,1]{1,0:T(1,128)}, f32[1,1]{1,0:T(1,128)}, /*index=5*/f32[1,1]{1,0:T(1,128)}) fusion(f32[1,6]{1,0:T(1,128)} %param.12), kind=kLoop, calls=%fused_computation.38 | loop fusion | bytes 48 | tf_op jit(solution)/shard_map/slice | solution.py:187
  3.8 3.8 %select_select_fusion.mech_ref = f32[8,128]{1,0:T(8,128)S(1)} fusion(f32[]{:T(128)} %bitcast.8, f32[]{:T(128)} %bitcast.7, f32[]{:T(128)} %bitcast.6, f32[]{:T(128)} %bitcast.5, f32[]{:T(128)} %bitcast.4, f32[]{:T(128)} %bitcast.3, s32[128]{0:T(128)S(1)} %get-tuple-element.15, s32[128]{0:T(128)S(1)} %get-tuple-element.16, s32[8]{0:T(128)S(1)} %get-tuple-element.13, ...), kind=kLoop, calls=%fused_computation.6 | loop fusion | flops 15360 | bytes 5976 | tf_op jit(solution)/shard_map/jit(_where)/select_n | solution.py:187
  7.6 0.1 iota_compare_fusion
  7.7 0.2 select_reduce_fusion
  7.9 2.5 %reshape.289.green_ref = bf16[16,48,1024]{2,1,0:T(8,128)(2,1)S(1)} reshape(bf16[16,4,6,2,1024]{4,3,2,1,0:T(2,128)(2,1)} %param.7) | data formatting | bytes 3145728 | tf_op jit(solution)/shard_map/reshape | solution.py:212
  10.4 0.0 copy-start
  10.4 0.0 copy-start.1
  10.4 0.0 copy-start.2
  10.4 34.8 %exchange.1 = f32[16,2,8,1024]{3,2,1,0:T(8,128)S(1)} custom-call(s32[16,1,128]{2,1,0:T(1,128)S(1)} %bitcast.30, f32[8,128]{1,0:T(8,128)S(1)} %select_select_fusion.mech_ref, bf16[16,48,1024]{2,1,0:T(8,128)(2,1)S(1)} %reshape.289.green_ref), custom_call_target="tpu_custom_call" | custom-call | tf_op jit(solution)/shard_map/exchange/pallas_call | solution.py:191
  45.2 0.0 copy-done
  45.2 0.0 copy-done.1
  45.2 0.0 copy-done.2
  45.2 17.0 %motion.1 = f32[16,2,1024]{2,1,0:T(2,128)} custom-call(s32[32]{0:T(128)S(1)} %multiply_add_fusion.rows_ref, s32[1]{0:T(128)S(6)} %copy.8.count_ref, f32[32,8,1024]{2,1,0:T(8,128)S(1)} %bitcast.29, s32[16,128]{1,0:T(8,128)S(1)} %bitcast.31, f32[16,128]{1,0:T(8,128)S(1)} %bitcast.32, f32[16,128]{1,0:T(8,128)S(1)} %bitcast.33), custom_call_target="tpu_custom_call" | custom-call | tf_op jit(solution)/shard_map/motion/pallas_call | solution.py:214
  (7 shorter events, 0.1 us)
Async XLA Ops:
  10.4 34.8 %copy-start = (s32[1,16,128]{2,1,0:T(8,128)S(1)}, s32[1,16,128]{2,1,0:T(8,128)}, u32[]{:S(2)}) copy-start(s32[1,16,128]{2,1,0:T(8,128)} %param.10) | copy-start | bytes 24580
  10.4 34.8 %copy-start.1 = (f32[1,16,128]{2,1,0:T(8,128)S(1)}, f32[1,16,128]{2,1,0:T(8,128)}, u32[]{:S(2)}) copy-start(f32[1,16,128]{2,1,0:T(8,128)} %param.11) | copy-start | bytes 24580
  10.4 34.8 %copy-start.2 = (f32[1,16,128]{2,1,0:T(8,128)S(1)}, f32[1,16,128]{2,1,0:T(8,128)}, u32[]{:S(2)}) copy-start(f32[1,16,128]{2,1,0:T(8,128)} %param.13) | copy-start | bytes 24580

commit v2 on v1

v2 whole, which is shorter than its diff:
```python
import functools

import jax
import jax.numpy as jnp
from jax import lax
from jax.experimental import pallas as pl
from jax.experimental.pallas import tpu as pltpu
from jax.sharding import PartitionSpec as P

LANES = 128


def seismogram_kernel(n, cap, points, comps, width, listed, wants_s_ref, mech_s_ref, count_ref,
                      wants_ref, green_ref, onset_ref, slip_ref, rate_ref, out_ref,
                      wanted, mech, mechs, wanted_s, outbox, out_scale, inbox, in_scale, traces,
                      motion, high_taps, low_taps,
                      send_w, recv_w, send_m, recv_m, local_sem, send_t, recv_t, send_s, recv_s):
    me = lax.axis_index("pts")
    rows = points * comps
    length = traces.shape[-1]
    tiles = length // LANES
    half = tiles // 2
    strains = width // rows
    variations = onset_ref.shape[0]
    mesh_id = pl.DeviceIdType.MESH
    lane = lax.broadcasted_iota(jnp.int32, (8, LANES), 1)
    sub = lax.broadcasted_iota(jnp.int32, (8, LANES), 0)

    barrier = pltpu.get_barrier_semaphore()

    def greet(d, carry):
        pl.semaphore_signal(barrier, inc=1, device_id={"pts": lax.rem(me + d, n)},
                            device_id_type=mesh_id)
        return carry

    lax.fori_loop(1, n, greet, 0)

    out_row = lax.broadcasted_iota(jnp.int32, (rows, LANES), 0)
    in_row = lax.broadcasted_iota(jnp.int32, (rows, LANES), 1)
    table = jnp.zeros((rows, LANES), jnp.float32)
    for p in range(points):
        for s in range(strains):
            for c in range(comps):
                here = (out_row == p * comps + c) & (in_row == (p * strains + s) * comps + c)
                table = jnp.where(here, mech_s_ref[0, s], table)
    mech[...] = table
    mechs[0] = table
    wanted[0] = wants_ref[me]
    pl.semaphore_wait(barrier, n - 1)

    def remote(src, dst, send, recv, d):
        return pltpu.make_async_remote_copy(
            src_ref=src, dst_ref=dst.at[n - d], send_sem=send.at[d], recv_sem=recv.at[n - d],
            device_id={"pts": lax.rem(me + d, n)}, device_id_type=mesh_id)

    def want_copy(d):
        return remote(wants_ref.at[lax.rem(me + d, n)], wanted, send_w, recv_w, d)

    def mech_copy(d):
        return remote(mech, mechs, send_m, recv_m, d)

    def trace_copy(d):
        return remote(outbox.at[d], inbox, send_t, recv_t, d)

    def scale_copy(d):
        return remote(out_scale.at[d], in_scale, send_s, recv_s, d)

    def start_meta(d, carry):
        want_copy(d).start()
        mech_copy(d).start()
        return carry

    lax.fori_loop(1, n, start_meta, 0)

    def wait_meta(d, carry):
        want_copy(d).wait()
        mech_copy(d).wait()
        return carry

    lax.fori_loop(1, n, wait_meta, 0)
    to_scalar = pltpu.make_async_copy(wanted, wanted_s, local_sem)
    to_scalar.start()
    to_scalar.wait()

    def encode(d, box, scale_box, at):
        lhs = mechs[d][:, :width]
        high = lhs.astype(jnp.bfloat16).astype(jnp.float32)
        rest = lhs - high
        mid = rest.astype(jnp.bfloat16).astype(jnp.float32)
        stack = jnp.concatenate([high, mid, rest - mid], axis=0).astype(jnp.bfloat16)
        scales = jnp.zeros((8, LANES), jnp.float32)
        for slot in range(cap):
            block = green_ref[wanted_s[d, 0, slot]]
            parts = jnp.dot(stack, block, preferred_element_type=jnp.float32)
            full = parts[0:rows] + (parts[rows:2 * rows] + parts[2 * rows:3 * rows])
            coded = []
            for i in range(tiles):
                part = full[:, i * LANES:(i + 1) * LANES]
                top = jnp.max(jnp.abs(part), axis=1, keepdims=True)
                inverse = 32767.0 / jnp.maximum(top, 1e-30)
                coded.append(jnp.floor(part * inverse + 0.5).astype(jnp.int32))
                scales = jnp.where(lane == (slot * tiles + i) * rows + sub,
                                   top * (1.0 / 32767.0), scales)
            for i in range(half):
                word = jnp.bitwise_or(jnp.left_shift(coded[i + half], 16),
                                      jnp.bitwise_and(coded[i], 0xFFFF))
                box[at, slot, :, i * LANES:(i + 1) * LANES] = word
        scale_box[at] = jnp.sum(scales, axis=0, keepdims=True)

    def send(d, carry):
        encode(d, outbox, out_scale, d)

        @pl.when(d > 1)
        def _():
            trace_copy(d - 1).start()
            scale_copy(d - 1).start()

        return carry

    lax.fori_loop(1, n, send, 0)
    encode(0, inbox, in_scale, 0)
    trace_copy(n - 1).start()
    scale_copy(n - 1).start()

    i_row = lax.broadcasted_iota(jnp.int32, (LANES, LANES), 0)
    j_lane = lax.broadcasted_iota(jnp.int32, (LANES, LANES), 1)
    near_mask = j_lane >= i_row
    motion[...] = jnp.zeros(motion.shape, jnp.float32)

    for v in range(variations):
        rate = jnp.broadcast_to(rate_ref[v:v + 1, :], (LANES, LANES))
        turned = pltpu.roll(rate, 0, 1, stride=1, stride_axis=0)
        both = jnp.concatenate(
            [jnp.where(near_mask, turned, 0.0), jnp.where(near_mask, 0.0, turned)], axis=0)
        high = both.astype(jnp.bfloat16)
        high_taps[v] = high
        low_taps[v] = (both - high.astype(jnp.float32)).astype(jnp.bfloat16)

    def arrive(step, carry):
        j = lax.rem(n - step, n)
        source_device = lax.rem(me + j, n)

        @pl.when(step > 0)
        def _():
            trace_copy(step).wait_recv()
            scale_copy(step).wait_recv()

        scales = jnp.broadcast_to(in_scale[j], (8, LANES))
        for slot in range(cap):
            for i in range(half):
                word = inbox[j, slot, :, i * LANES:(i + 1) * LANES]
                low = jnp.right_shift(jnp.left_shift(word, 16), 16)
                high = jnp.right_shift(word, 16)
                for at, value in ((i, low), (i + half, high)):
                    scale = jnp.take_along_axis(scales, (slot * tiles + at) * rows + sub, axis=1)
                    traces[slot, :, at * LANES:(at + 1) * LANES] = (
                        value.astype(jnp.float32) * scale)
        for group in range(variations // 8):
            onsets = onset_ref[group * 8:group * 8 + 8, :]
            slips = slip_ref[group * 8:group * 8 + 8, :]
            acc = [motion[comps + q, group * 8:group * 8 + 8, :] for q in range(tiles * comps)]
            for slot in range(cap):
                k = wants_s_ref[source_device, 0, cap + slot]
                used = jnp.where(jnp.full((8, LANES), k, jnp.int32) < count_ref[0], 1.0, 0.0)
                base = jnp.minimum(jnp.full((8, LANES), k, jnp.int32), listed - 1) * points
                for p in range(points):
                    onset = jnp.take_along_axis(onsets, base + p, axis=1)
                    slip = jnp.take_along_axis(slips, base + p, axis=1) * used
                    shift = jnp.bitwise_and(onset, LANES - 1)
                    back = jnp.right_shift(onset, 7) + (lane >= LANES - shift).astype(jnp.int32)
                    one = back >= 1
                    two = back >= 2
                    source = jnp.bitwise_and(lane - shift, LANES - 1)
                    for c in range(comps):
                        prev2 = jnp.zeros((8, LANES), jnp.float32)
                        prev1 = prev2
                        for i in range(tiles):
                            cur = jnp.broadcast_to(
                                traces[slot, p * comps + c:p * comps + c + 1,
                                       i * LANES:(i + 1) * LANES], (8, LANES))
                            mixed = jnp.where(two, prev2, jnp.where(one, prev1, cur))
                            acc[i * comps + c] += slip * jnp.take_along_axis(mixed, source, axis=1)
                            prev2, prev1 = prev1, cur
            for q in range(tiles * comps):
                motion[comps + q, group * 8:group * 8 + 8, :] = acc[q]
        return carry

    lax.fori_loop(0, n, arrive, 0)

    count = tiles * comps
    for v in range(variations):
        lhs = jnp.concatenate([motion[comps:comps + count, v, :], motion[0:count, v, :]], axis=1)
        high = lhs.astype(jnp.bfloat16).astype(jnp.float32)
        pair = jnp.concatenate([high, lhs - high], axis=0).astype(jnp.bfloat16)
        main = jnp.dot(pair, high_taps[v], preferred_element_type=jnp.float32)
        minor = jnp.dot(pair[:count], low_taps[v], preferred_element_type=jnp.float32)
        result = main[:count] + (main[count:] + minor)
        for i in range(tiles):
            out_ref[v, :, i * LANES:(i + 1) * LANES] = result[i * comps:(i + 1) * comps, :]

    def wait_sent(d, carry):
        trace_copy(d).wait_send()
        scale_copy(d).wait_send()
        return carry

    lax.fori_loop(1, n, wait_sent, 0)


def local(green_tensors, block_lists, block_count, onset_steps, slip_amount, mechanism, slip_rate):
    held, points, strains, comps, length = green_tensors.shape
    ruptures, listed = block_lists.shape
    assert ruptures == 1
    variations = onset_steps.shape[1]
    n = lax.axis_size("pts")
    cap = max(1, listed // n)
    width = points * strains * comps
    rows = points * comps
    tiles = length // LANES
    assert cap * tiles * rows <= LANES

    blocks = block_lists.reshape(listed)
    holder = blocks // held
    order = jnp.arange(listed, dtype=jnp.int32)
    rank = jnp.sum(((holder[:, None] == holder[None, :]) & (order[None, :] < order[:, None]))
                   .astype(jnp.int32), axis=1)
    lanes = jnp.arange(LANES, dtype=jnp.int32)
    hit = (holder[None, None, :] == jnp.arange(n, dtype=jnp.int32)[:, None, None]) & (
        rank[None, None, :] == (lanes % cap)[None, :, None])
    value = jnp.where((lanes < cap)[None, :, None], (blocks % held)[None, None, :],
                      (order - listed)[None, None, :])
    wants = jnp.sum(jnp.where(hit, value, 0), axis=2) + jnp.where(lanes < cap, 0, listed)[None, :]
    wants = wants.astype(jnp.int32).reshape(n, 1, LANES)

    vmem = pl.BlockSpec(memory_space=pltpu.VMEM)
    smem = pl.BlockSpec(memory_space=pltpu.SMEM)
    dma = pltpu.SemaphoreType.DMA
    seismograms = pl.pallas_call(
        functools.partial(seismogram_kernel, n, cap, points, comps, width, listed),
        out_shape=jax.ShapeDtypeStruct((variations, comps, length), jnp.float32),
        in_specs=[smem, smem, smem, vmem, vmem, vmem, vmem, vmem],
        out_specs=vmem,
        scratch_shapes=[
            pltpu.VMEM((n, 1, LANES), jnp.int32),
            pltpu.VMEM((rows, LANES), jnp.float32),
            pltpu.VMEM((n, rows, LANES), jnp.float32),
            pltpu.SMEM((n, 1, LANES), jnp.int32),
            pltpu.VMEM((n, cap, rows, length // 2), jnp.int32),
            pltpu.VMEM((n, 1, LANES), jnp.float32),
            pltpu.VMEM((n, cap, rows, length // 2), jnp.int32),
            pltpu.VMEM((n, 1, LANES), jnp.float32),
            pltpu.VMEM((cap, rows, length), jnp.float32),
            pltpu.VMEM(((tiles + 1) * comps, variations, LANES), jnp.float32),
            pltpu.VMEM((variations, 2 * LANES, LANES), jnp.bfloat16),
            pltpu.VMEM((variations, 2 * LANES, LANES), jnp.bfloat16),
            dma((n,)), dma((n,)), dma((n,)), dma((n,)), dma,
            dma((n,)), dma((n,)), dma((n,)), dma((n,)),
        ],
        compiler_params=pltpu.CompilerParams(
            collective_id=0, has_side_effects=True, vmem_limit_bytes=48 << 20),
        name="seismograms",
    )(wants, mechanism, block_count, wants, green_tensors.reshape(held, width, length),
      onset_steps[0], slip_amount[0], slip_rate[0])
    return seismograms[None]


def solution(mesh):
    in_specs = (
        P(("site", "pts"), None, None, None, None),
        P(("site", "pts"), None),
        P(("site", "pts")),
        P(("site", "pts"), None, None),
        P(("site", "pts"), None, None),
        P(("site", "pts"), None),
        P(("site", "pts"), None, None),
    )
    out_specs = P(("site", "pts"), None, None, None)
    return jax.shard_map(local, mesh=mesh, in_specs=in_specs, out_specs=out_specs, check_vma=False)
```

time: 62.5 us -> 44.5 us (0.71)
  the two profiles are of different devices: /device:TPU:15 before, /device:TPU:0 now
where the time goes in v2:
time: 44.5 us; the launch traced here: 44.2 us
  Pallas kernels  38.4 us (86%)
  local copies, waits for them, and re-layouts  3.2 us (7%)
  other arithmetic  1.84 us (4%)
  between operations  0.77 us (2%)
    pallas_call x1, Pallas kernels, local(): pl.pallas_call(functools.partial(seismogram_kernel, n, cap, points, comps...  38.4 us
    reshape x1, local copies, waits for them, and re-layouts, local(): green_tensors.reshape(held, width, length)  2.51 us

profile of v2, /device:TPU:0, one launch (start us, length us, event | category | flops | bytes accessed | tf_op | source)
XLA Modules:
  0.0 44.2 jit_solution(9691469422819423379)
XLA Ops:
  0.7 0.7 %fusion.1 = s32[32]{0:T(128)S(1)} fusion(s32[1,32]{1,0:T(1,128)} %param.8), kind=kLoop, calls=%fused_computation.21 | loop fusion | flops 480 | bytes 256 | tf_op jit(solution)/shard_map/eq | solution.py:224
  1.3 0.7 %and_select_fusion.3 = (s32[32]{0:T(128)S(1)}, s32[32]{0:T(128)S(1)}, s32[32]{0:T(128)S(1)}) fusion(s32[1,32]{1,0:T(1,128)} %param.8), kind=kLoop, calls=%fused_computation.11 | loop fusion | flops 640 | bytes 512 | tf_op jit(solution)/shard_map/jit(floor_divide)/jit(_where)/select_n | solution.py:222
  2.0 0.2 convert_reduce_fusion
  2.2 0.1 broadcast_compare_fusion
  2.3 0.1 broadcast_select_fusion
  2.3 0.2 select_reduce_fusion
  2.5 0.0 copy-start
  2.5 0.0 copy-start.1
  2.6 0.0 copy-start.2
  2.6 0.0 copy-start.3
  2.6 2.5 %reshape.235.green_ref = bf16[16,48,1024]{2,1,0:T(8,128)(2,1)S(1)} reshape(bf16[16,4,6,2,1024]{4,3,2,1,0:T(2,128)(2,1)} %param.7) | data formatting | bytes 3145728 | tf_op jit(solution)/shard_map/reshape | solution.py:261
  5.1 0.0 copy-done
  5.1 0.0 copy-done.1
  5.1 0.0 copy-done.2
  5.1 0.0 copy-done.3
  5.1 38.4 %seismograms.1 = f32[16,2,1024]{2,1,0:T(2,128)S(1)} custom-call(s32[16,1,128]{2,1,0:T(1,128)S(1)} %broadcast_add_fusion.wants_s_ref.wants_ref, f32[1,6]{1,0:T(1,128)S(1)} %copy-done.3, s32[1]{0:T(128)S(6)} %copy.9.count_ref, s32[16,1,128]{2,1,0:T(1,128)S(1)} %broadcast_add_fusion.wants_s_ref.wants_ref, bf16[16,48,1024]{2,1,0:T(8,128)(2,1)S(1)} %reshape.235.green_ref, ...), custom_call_target="tpu_custom_call" | custom-call | tf_op jit(solution)/shard_map/seismograms/pallas_call | solution.py:237
  43.6 0.7 %copy.10 = f32[1,16,2,1024]{3,2,1,0:T(2,128)} copy(f32[1,16,2,1024]{3,2,1,0:T(2,128)S(1)} %bitcast.22) | data formatting | bytes 262144
  (5 shorter events, 0.0 us)
Async XLA Ops:
  2.5 2.6 %copy-start = (s32[1,16,128]{2,1,0:T(8,128)S(1)}, s32[1,16,128]{2,1,0:T(8,128)}, u32[]{:S(2)}) copy-start(s32[1,16,128]{2,1,0:T(8,128)} %param.10) | copy-start | bytes 24580
  2.5 2.6 %copy-start.1 = (f32[1,16,128]{2,1,0:T(8,128)S(1)}, f32[1,16,128]{2,1,0:T(8,128)}, u32[]{:S(2)}) copy-start(f32[1,16,128]{2,1,0:T(8,128)} %param.11) | copy-start | bytes 24580
  2.6 2.6 %copy-start.2 = (f32[1,16,128]{2,1,0:T(8,128)S(1)}, f32[1,16,128]{2,1,0:T(8,128)}, u32[]{:S(2)}) copy-start(f32[1,16,128]{2,1,0:T(8,128)} %param.13) | copy-start | bytes 24580
  2.6 2.6 %copy-start.3 = (f32[1,6]{1,0:T(1,128)S(1)}, f32[1,6]{1,0:T(1,128)}, u32[]{:S(2)}) copy-start(f32[1,6]{1,0:T(1,128)} %mech_s_ref.1) | copy-start | bytes 76

commit v3 on v2

--- a/solution.py
+++ b/solution.py
@@ -12,12 +12,12 @@
 
 def seismogram_kernel(n, cap, points, comps, width, listed, wants_s_ref, mech_s_ref, count_ref,
                       wants_ref, green_ref, onset_ref, slip_ref, rate_ref, out_ref,
-                      wanted, mech, mechs, wanted_s, outbox, out_scale, inbox, in_scale, traces,
-                      motion, high_taps, low_taps,
+                      wanted, mech, mechs, wanted_s, outbox, out_scale, inbox, in_scale,
+                      motion, high_taps, low_taps, onset_of, slip_of,
                       send_w, recv_w, send_m, recv_m, local_sem, send_t, recv_t, send_s, recv_s):
     me = lax.axis_index("pts")
     rows = points * comps
-    length = traces.shape[-1]
+    length = out_ref.shape[-1]
     tiles = length // LANES
     half = tiles // 2
     strains = width // rows
@@ -72,6 +72,28 @@
 
     lax.fori_loop(1, n, start_meta, 0)
 
+    i_row = lax.broadcasted_iota(jnp.int32, (LANES, LANES), 0)
+    j_lane = lax.broadcasted_iota(jnp.int32, (LANES, LANES), 1)
+    near_mask = j_lane >= i_row
+    motion[...] = jnp.zeros(motion.shape, jnp.float32)
+
+    for v in range(variations):
+        rate = jnp.broadcast_to(rate_ref[v:v + 1, :], (LANES, LANES))
+        turned = pltpu.roll(rate, 0, 1, stride=1, stride_axis=0)
+        both = jnp.concatenate(
+            [jnp.where(near_mask, turned, 0.0), jnp.where(near_mask, 0.0, turned)], axis=0)
+        high = both.astype(jnp.bfloat16)
+        high_taps[v] = high
+        low_taps[v] = (both - high.astype(jnp.float32)).astype(jnp.bfloat16)
+
+    def spread(q, carry):
+        pick = jnp.full((variations, LANES), q, jnp.int32)
+        onset_of[q] = jnp.take_along_axis(onset_ref[...], pick, axis=1)
+        slip_of[q] = jnp.take_along_axis(slip_ref[...], pick, axis=1)
+        return carry
+
+    lax.fori_loop(0, listed * points, spread, 0, unroll=4)
+
     def wait_meta(d, carry):
         want_copy(d).wait()
         mech_copy(d).wait()
@@ -93,14 +115,14 @@
             block = green_ref[wanted_s[d, 0, slot]]
             parts = jnp.dot(stack, block, preferred_element_type=jnp.float32)
             full = parts[0:rows] + (parts[rows:2 * rows] + parts[2 * rows:3 * rows])
-            coded = []
-            for i in range(tiles):
-                part = full[:, i * LANES:(i + 1) * LANES]
-                top = jnp.max(jnp.abs(part), axis=1, keepdims=True)
-                inverse = 32767.0 / jnp.maximum(top, 1e-30)
-                coded.append(jnp.floor(part * inverse + 0.5).astype(jnp.int32))
-                scales = jnp.where(lane == (slot * tiles + i) * rows + sub,
-                                   top * (1.0 / 32767.0), scales)
+            cut = [full[:, i * LANES:(i + 1) * LANES] for i in range(tiles)]
+            top = jnp.abs(cut[0])
+            for part in cut[1:]:
+                top = jnp.maximum(top, jnp.abs(part))
+            top = jnp.max(top, axis=1, keepdims=True)
+            inverse = 32767.0 / jnp.maximum(top, 1e-30)
+            coded = [jnp.floor(part * inverse + 0.5).astype(jnp.int32) for part in cut]
+            scales = jnp.where(lane == slot * rows + sub, top * (1.0 / 32767.0), scales)
             for i in range(half):
                 word = jnp.bitwise_or(jnp.left_shift(coded[i + half], 16),
                                       jnp.bitwise_and(coded[i], 0xFFFF))
@@ -122,20 +144,6 @@
     trace_copy(n - 1).start()
     scale_copy(n - 1).start()
 
-    i_row = lax.broadcasted_iota(jnp.int32, (LANES, LANES), 0)
-    j_lane = lax.broadcasted_iota(jnp.int32, (LANES, LANES), 1)
-    near_mask = j_lane >= i_row
-    motion[...] = jnp.zeros(motion.shape, jnp.float32)
-
-    for v in range(variations):
-        rate = jnp.broadcast_to(rate_ref[v:v + 1, :], (LANES, LANES))
-        turned = pltpu.roll(rate, 0, 1, stride=1, stride_axis=0)
-        both = jnp.concatenate(
-            [jnp.where(near_mask, turned, 0.0), jnp.where(near_mask, 0.0, turned)], axis=0)
-        high = both.astype(jnp.bfloat16)
-        high_taps[v] = high
-        low_taps[v] = (both - high.astype(jnp.float32)).astype(jnp.bfloat16)
-
     def arrive(step, carry):
         j = lax.rem(n - step, n)
         source_device = lax.rem(me + j, n)
@@ -146,40 +154,38 @@
             scale_copy(step).wait_recv()
 
         scales = jnp.broadcast_to(in_scale[j], (8, LANES))
-        for slot in range(cap):
-            for i in range(half):
-                word = inbox[j, slot, :, i * LANES:(i + 1) * LANES]
-                low = jnp.right_shift(jnp.left_shift(word, 16), 16)
-                high = jnp.right_shift(word, 16)
-                for at, value in ((i, low), (i + half, high)):
-                    scale = jnp.take_along_axis(scales, (slot * tiles + at) * rows + sub, axis=1)
-                    traces[slot, :, at * LANES:(at + 1) * LANES] = (
-                        value.astype(jnp.float32) * scale)
+        scale_of = [jnp.take_along_axis(scales, jnp.full((8, LANES), q, jnp.int32), axis=1)
+                    for q in range(cap * rows)]
         for group in range(variations // 8):
-            onsets = onset_ref[group * 8:group * 8 + 8, :]
-            slips = slip_ref[group * 8:group * 8 + 8, :]
             acc = [motion[comps + q, group * 8:group * 8 + 8, :] for q in range(tiles * comps)]
             for slot in range(cap):
                 k = wants_s_ref[source_device, 0, cap + slot]
                 used = jnp.where(jnp.full((8, LANES), k, jnp.int32) < count_ref[0], 1.0, 0.0)
-                base = jnp.minimum(jnp.full((8, LANES), k, jnp.int32), listed - 1) * points
+                base = jnp.minimum(k, listed - 1) * points
                 for p in range(points):
-                    onset = jnp.take_along_axis(onsets, base + p, axis=1)
-                    slip = jnp.take_along_axis(slips, base + p, axis=1) * used
+                    onset = onset_of[base + p, group * 8:group * 8 + 8, :]
+                    slip = slip_of[base + p, group * 8:group * 8 + 8, :] * used
                     shift = jnp.bitwise_and(onset, LANES - 1)
                     back = jnp.right_shift(onset, 7) + (lane >= LANES - shift).astype(jnp.int32)
                     one = back >= 1
                     two = back >= 2
                     source = jnp.bitwise_and(lane - shift, LANES - 1)
                     for c in range(comps):
-                        prev2 = jnp.zeros((8, LANES), jnp.float32)
-                        prev1 = prev2
-                        for i in range(tiles):
-                            cur = jnp.broadcast_to(
-                                traces[slot, p * comps + c:p * comps + c + 1,
-                                       i * LANES:(i + 1) * LANES], (8, LANES))
+                        row = p * comps + c
+                        weight = slip * scale_of[slot * rows + row]
+                        words = [jnp.broadcast_to(
+                            inbox[j, slot, row:row + 1, i * LANES:(i + 1) * LANES], (8, LANES))
+                            for i in range(half)]
+                        prev2 = jnp.left_shift(words[half - 2], 16)
+                        prev1 = jnp.left_shift(words[half - 1], 16)
+                        for i in range(half):
+                            cur = words[i]
                             mixed = jnp.where(two, prev2, jnp.where(one, prev1, cur))
-                            acc[i * comps + c] += slip * jnp.take_along_axis(mixed, source, axis=1)
+                            moved = jnp.take_along_axis(mixed, source, axis=1)
+                            low = jnp.right_shift(jnp.left_shift(moved, 16), 16)
+                            high = jnp.right_shift(moved, 16)
+                            acc[i * comps + c] += weight * low.astype(jnp.float32)
+                            acc[(i + half) * comps + c] += weight * high.astype(jnp.float32)
                             prev2, prev1 = prev1, cur
             for q in range(tiles * comps):
                 motion[comps + q, group * 8:group * 8 + 8, :] = acc[q]
@@ -216,7 +222,7 @@
     width = points * strains * comps
     rows = points * comps
     tiles = length // LANES
-    assert cap * tiles * rows <= LANES
+    assert cap * rows <= LANES
 
     blocks = block_lists.reshape(listed)
     holder = blocks // held
@@ -248,10 +254,11 @@
             pltpu.VMEM((n, 1, LANES), jnp.float32),
             pltpu.VMEM((n, cap, rows, length // 2), jnp.int32),
             pltpu.VMEM((n, 1, LANES), jnp.float32),
-            pltpu.VMEM((cap, rows, length), jnp.float32),
             pltpu.VMEM(((tiles + 1) * comps, variations, LANES), jnp.float32),
             pltpu.VMEM((variations, 2 * LANES, LANES), jnp.bfloat16),
             pltpu.VMEM((variations, 2 * LANES, LANES), jnp.bfloat16),
+            pltpu.VMEM((listed * points, variations, LANES), jnp.int32),
+            pltpu.VMEM((listed * points, variations, LANES), jnp.float32),
             dma((n,)), dma((n,)), dma((n,)), dma((n,)), dma,
             dma((n,)), dma((n,)), dma((n,)), dma((n,)),
         ],

time: 44.5 us -> 33 us (0.74)
  Pallas kernels: 38.4 us -> 27 us
    pallas_call x1, Pallas kernels: 38.4 us -> 27 us  [local(): pl.pallas_call(functools.partial(seismogram_kernel, n, cap, points, comps...]
where the time goes in v3:
time: 33 us; the launch traced here: 32.8 us
  Pallas kernels  27 us (82%)
  local copies, waits for them, and re-layouts  3.2 us (10%)
  other arithmetic  1.84 us (6%)
  between operations  0.77 us (2%)
    pallas_call x1, Pallas kernels, local(): pl.pallas_call(functools.partial(seismogram_kernel, n, cap, points, comps...  27 us
    reshape x1, local copies, waits for them, and re-layouts, local(): green_tensors.reshape(held, width, length)  2.51 us
    unnamed x9, local copies, waits for them, and re-layouts  0.68 us
    select_n x1, other arithmetic, local(): holder = blocks // held  0.67 us
    eq x1, other arithmetic, local(): holder[:, None] == holder[None, :]  0.67 us

profile of v3, /device:TPU:0, one launch (start us, length us, event | category | flops | bytes accessed | tf_op | source)
XLA Modules:
  0.0 32.8 jit_solution(11418771367258473857)
XLA Ops:
  0.7 0.7 %fusion.1 = s32[32]{0:T(128)S(1)} fusion(s32[1,32]{1,0:T(1,128)} %param.8), kind=kLoop, calls=%fused_computation.21 | loop fusion | flops 480 | bytes 256 | tf_op jit(solution)/shard_map/eq | solution.py:230
  1.3 0.7 %and_select_fusion.3 = (s32[32]{0:T(128)S(1)}, s32[32]{0:T(128)S(1)}, s32[32]{0:T(128)S(1)}) fusion(s32[1,32]{1,0:T(1,128)} %param.8), kind=kLoop, calls=%fused_computation.11 | loop fusion | flops 640 | bytes 512 | tf_op jit(solution)/shard_map/jit(floor_divide)/jit(_where)/select_n | solution.py:228
  2.0 0.2 convert_reduce_fusion
  2.2 0.1 broadcast_compare_fusion
  2.3 0.1 broadcast_select_fusion
  2.3 0.2 select_reduce_fusion
  2.5 0.0 copy-start
  2.5 0.0 copy-start.1
  2.6 0.0 copy-start.2
  2.6 0.0 copy-start.3
  2.6 2.5 %reshape.235.green_ref = bf16[16,48,1024]{2,1,0:T(8,128)(2,1)S(1)} reshape(bf16[16,4,6,2,1024]{4,3,2,1,0:T(2,128)(2,1)} %param.7) | data formatting | bytes 3145728 | tf_op jit(solution)/shard_map/reshape | solution.py:268
  5.1 0.0 copy-done
  5.1 0.0 copy-done.1
  5.1 0.0 copy-done.2
  5.1 0.0 copy-done.3
  5.1 27.0 %seismograms.1 = f32[16,2,1024]{2,1,0:T(2,128)S(1)} custom-call(s32[16,1,128]{2,1,0:T(1,128)S(1)} %broadcast_add_fusion.wants_s_ref.wants_ref, f32[1,6]{1,0:T(1,128)S(1)} %copy-done.3, s32[1]{0:T(128)S(6)} %copy.9.count_ref, s32[16,1,128]{2,1,0:T(1,128)S(1)} %broadcast_add_fusion.wants_s_ref.wants_ref, bf16[16,48,1024]{2,1,0:T(8,128)(2,1)S(1)} %reshape.235.green_ref, ...), custom_call_target="tpu_custom_call" | custom-call | tf_op jit(solution)/shard_map/seismograms/pallas_call | solution.py:243
  32.1 0.7 %copy.10 = f32[1,16,2,1024]{3,2,1,0:T(2,128)} copy(f32[1,16,2,1024]{3,2,1,0:T(2,128)S(1)} %bitcast.22) | data formatting | bytes 262144
  (5 shorter events, 0.0 us)
Async XLA Ops:
  2.5 2.6 %copy-start = (s32[1,16,128]{2,1,0:T(8,128)S(1)}, s32[1,16,128]{2,1,0:T(8,128)}, u32[]{:S(2)}) copy-start(s32[1,16,128]{2,1,0:T(8,128)} %param.10) | copy-start | bytes 24580
  2.5 2.6 %copy-start.1 = (f32[1,16,128]{2,1,0:T(8,128)S(1)}, f32[1,16,128]{2,1,0:T(8,128)}, u32[]{:S(2)}) copy-start(f32[1,16,128]{2,1,0:T(8,128)} %param.11) | copy-start | bytes 24580
  2.6 2.6 %copy-start.2 = (f32[1,16,128]{2,1,0:T(8,128)S(1)}, f32[1,16,128]{2,1,0:T(8,128)}, u32[]{:S(2)}) copy-start(f32[1,16,128]{2,1,0:T(8,128)} %param.13) | copy-start | bytes 24580
  2.6 2.6 %copy-start.3 = (f32[1,6]{1,0:T(1,128)S(1)}, f32[1,6]{1,0:T(1,128)}, u32[]{:S(2)}) copy-start(f32[1,6]{1,0:T(1,128)} %mech_s_ref.1) | copy-start | bytes 76
